TPU v7x, 128 devices: a whole 4x4x4 slice. The times are simulated.
128 devices in a mesh: seq: 32 (over x, z, core), res: 4 (over y).
Axes of the slice: x: 4, y: 4, z: 4, core: 2. Of those that a mesh axis runs over, the one named last changes fastest.
Arguments:
- alignment: bfloat16 [512, 4, 512, 256], P('seq', 'res'), may hold values from -8 to 8
- gain_attn: float32 [256], replicated, may hold values from 0.1 to 1.9
- w_proj: bfloat16 [256, 4, 256], replicated, may hold values from -0.75 to 0.75
- w_out: bfloat16 [256, 256], replicated, may hold values from -0.375 to 0.375
- gain_head: float32 [256], replicated, may hold values from 0.1 to 1.9
- w_head: bfloat16 [256, 23], replicated, may hold values from -1 to 1
- masked: int32 [512, 4, 512], P('res', None, 'seq'), may hold values from 0 to 1
- labels: int32 [512, 4, 512], P('res', None, 'seq'), may hold values from 0 to 22
Outputs:
- updated: bfloat16 [512, 4, 512, 256], P('res', None, 'seq')
- masked_loss: float32 [], replicated
- mask_share: float32 [], replicated
All inputs are finite; a program needn't handle non-finite values.
Results may differ from a plain program's by a relative error of at most 0.011.
Values may be sent and summed in bfloat16 or wider, within the bound.
A program may use at most 192 MiB of HBM per device.

v0:
```python
import functools

import jax
import jax.numpy as jnp
from jax import lax
from jax.sharding import Mesh
from jax.sharding import PartitionSpec as P

HEADS = 8
HEAD_DIM = 32
SEQ = ("seq_0", "seq_1", "seq_2")
SEQ_RES = ("seq_0", "seq_1", "seq_2", "res")


def split_up(array, dim, devices):
    dims = array.shape
    parts = array.reshape(*dims[:dim], devices, dims[dim] // devices, *dims[dim + 1 :])
    return jnp.moveaxis(parts, dim, 0)


def edges_of(length, count):
    unit = 8 if length >= 8 * count else 1
    return [length // unit * k // count * unit for k in range(1, count)]


def joined_along(parts, dim):
    parts = jnp.moveaxis(parts, 0, dim)
    dims = parts.shape
    return parts.reshape(*dims[:dim], dims[dim] * dims[dim + 1], *dims[dim + 2 :])


def exchange_in_pieces(array, axis, pieces, split_dim, concat_dim):
    parts = split_up(array, split_dim, lax.axis_size(axis))
    split_at = max(range(1, max(2, parts.ndim - 1)), key=lambda d: parts.shape[d])
    done = []
    for piece in jnp.split(parts, edges_of(parts.shape[split_at], pieces), axis=split_at):
        if piece.size:
            done.append(lax.all_to_all(piece, axis, split_axis=0, concat_axis=0, tiled=True))
    return joined_along(jnp.concatenate(done, axis=split_at), concat_dim)


def over_axes(array, axes):
    return functools.reduce(lax.psum, axes, array)


def normalize(values, gain):
    mean = jnp.mean(values, axis=-1, keepdims=True)
    centred = values - mean
    spread = jnp.mean(centred * centred, axis=-1, keepdims=True)
    return centred * lax.rsqrt(spread + 1e-05) * gain


def project(flat_rows, gain_attn, w_proj):
    features = flat_rows.shape[1]
    normed = normalize(flat_rows.astype(jnp.float32), gain_attn).astype(jnp.bfloat16)
    return jnp.dot(
        normed, w_proj.reshape(features, 4 * features), preferred_element_type=jnp.float32
    ).astype(jnp.bfloat16)


def column_attention(queries, key_part, value_part):
    inv_root = HEAD_DIM ** (-0.5)
    scores = (
        jnp.einsum("shd,thd->hst", queries, key_part, preferred_element_type=jnp.float32) * inv_root
    )
    probs = jnp.exp(scores)
    totals = jnp.sum(probs, axis=2)
    weighted = jnp.einsum(
        "hst,thd->shd", probs.astype(jnp.bfloat16), value_part, preferred_element_type=jnp.float32
    )
    return (weighted, totals)


def finish(flat_rows, gated, w_out):
    summed = flat_rows.astype(jnp.float32) + jnp.dot(
        gated, w_out, preferred_element_type=jnp.float32
    )
    return summed.astype(jnp.bfloat16)


def on_device(alignment, gain_attn, w_proj, w_out, gain_head, w_head, masked, labels):
    weights = masked.reshape(-1).astype(jnp.float32)
    local_count = jnp.sum(weights)
    local_rows, single_block, segment, features = alignment.shape
    seq_devices = lax.axis_size(SEQ)
    split_view = alignment.reshape(local_rows, seq_devices, segment // seq_devices, features)
    column_block = lax.all_to_all(split_view, SEQ, split_axis=1, concat_axis=0, tiled=True)
    seq_total, single, col_count, features = column_block.shape
    by_column = jnp.transpose(column_block.reshape(seq_total, col_count, features), (1, 0, 2))
    flat_rows = by_column.reshape(col_count * seq_total, features)
    projected = project(flat_rows, gain_attn, w_proj).reshape(
        col_count, seq_total, 4, HEADS, HEAD_DIM
    )

    def per_column(picked):
        weighted, totals = column_attention(picked[:, 0], picked[:, 1], picked[:, 2])
        attended = weighted / totals.T[:, :, None]
        gated_col = attended * jax.nn.sigmoid(picked[:, 3].astype(jnp.float32))
        return gated_col.reshape(seq_total, features).astype(jnp.bfloat16)

    gated = lax.map(per_column, projected).reshape(col_count * seq_total, features)
    result = finish(flat_rows, gated, w_out).reshape(col_count, seq_total, features)
    result = jnp.transpose(result, (1, 0, 2)).reshape(seq_total, single, col_count, features)
    updated = exchange_in_pieces(result, "res", 2, 0, 1)
    features = updated.shape[3]
    flat_out = updated.reshape(-1, features)
    head_in = normalize(flat_out.astype(jnp.float32), gain_head).astype(jnp.bfloat16)
    logits = jnp.einsum("rc,ck->kr", head_in, w_head, preferred_element_type=jnp.float32)
    log_total = jnp.log(jnp.sum(jnp.exp(logits), axis=0))
    classes = jnp.arange(logits.shape[0], dtype=jnp.int32)[:, None]
    picked = jnp.sum(jnp.where(classes == labels.reshape(1, -1), logits, 0.0), axis=0)
    errors = log_total - picked
    local_loss = jnp.sum(errors * weights)
    loss_sum, mask_count = (over_axes(local_loss, SEQ_RES), over_axes(local_count, SEQ_RES))
    entries = flat_out.shape[0] * lax.axis_size(SEQ) * lax.axis_size("res")
    masked_loss = loss_sum / (1.0 + mask_count)
    mask_share = mask_count / entries
    return (updated, masked_loss, mask_share)


def solution(mesh):
    split = Mesh(
        mesh.devices.reshape(4, 4, 2, mesh.shape["res"]), ("seq_0", "seq_1", "seq_2", "res")
    )
    return jax.shard_map(
        on_device,
        mesh=split,
        in_specs=(
            P(SEQ, "res", None, None),
            P(),
            P(),
            P(),
            P(),
            P(),
            P("res", None, SEQ),
            P("res", None, SEQ),
        ),
        out_specs=(P("res", None, SEQ, None), P(), P()),
        check_vma=False,
    )
```

profile of v0, /device:TPU:1, one launch (start us, length us, event | category | flops | bytes accessed | tf_op | source)
XLA Modules:
  0.0 366.5 jit_solution(9256991756778645764)
XLA Ops:
  0.6 4.8 %copy.71 = bf16[16,32,16,256]{3,2,0,1:T(8,128)(2,1)} copy(bf16[16,32,16,256]{3,2,1,0:T(8,128)(2,1)} %bitcast.113) | data formatting | bytes 8388608 | tf_op jit(solution)/shard_map/reshape | solution.py:86
  5.4 9.6 %all-to-all-start = ((bf16[16,32,16,256]{3,2,0,1:T(8,128)(2,1)}), bf16[16,32,16,256]{3,2,0,1:T(8,128)(2,1)}, u32[]{:S(2)}, u32[]{:S(2)}) async-start(bf16[16,32,16,256]{3,2,0,1:T(8,128)(2,1)} %copy.71), calls=%async_computation | async-start | bytes 8388608 | tf_op jit(solution)/shard_map/all_to_all | solution.py:87
  15.2 52.0 %all-to-all-done = bf16[16,32,16,256]{3,2,0,1:T(8,128)(2,1)} async-done(((bf16[16,32,16,256]{3,2,0,1:T(8,128)(2,1)}), bf16[16,32,16,256]{3,2,0,1:T(8,128)(2,1)}, u32[]{:S(2)}, u32[]{:S(2)}) %all-to-all-start) | async-done | bytes 4194336 | tf_op jit(solution)/shard_map/all_to_all | solution.py:87
  67.2 3.4 bitcast_convert_fusion
  70.6 4.4 %bitcast_reduce_fusion = f32[16,512]{1,0:T(8,128)S(1)} fusion(f32[512,16,256]{2,1,0:T(8,128)S(1)} %bitcast.101), kind=kLoop, calls=%fused_computation.24 | loop fusion | flops 2088960 | bytes 8421376 | tf_op jit(solution)/shard_map/reduce_sum | solution.py:47
  75.0 8.1 %copy.72 = f32[512,16,256]{2,0,1:T(8,128)} copy(f32[512,16,256]{2,1,0:T(8,128)S(1)} %bitcast.102) | data formatting | bytes 16777216 | tf_op jit(solution)/shard_map/convert_element_type | solution.py:75
  83.1 6.5 %multiply_reduce_fusion.1 = f32[16,512]{1,0:T(8,128)S(1)} fusion(f32[16,512]{1,0:T(8,128)S(1)} %broadcast_multiply_fusion.1, f32[512,16,256]{2,1,0:T(8,128)S(1)} %bitcast.103), kind=kLoop, calls=%fused_computation.28 | loop fusion | flops 6283264 | bytes 8454144 | tf_op jit(solution)/shard_map/reduce_sum | solution.py:49
  89.6 6.4 %multiply_convert_fusion = bf16[16,512,256]{2,1,0:T(8,128)(2,1)} fusion(f32[256]{0:T(256)S(1)} %copy-done.4, f32[16,512]{1,0:T(8,128)S(1)} %add_rsqrt_fusion.1, f32[16,512]{1,0:T(8,128)S(1)} %broadcast_multiply_fusion.1, f32[512,16,256]{2,1,0:T(8,128)S(1)} %bitcast.104), kind=kLoop, calls=%fused_computation.27 | loop fusion | flops 8388608 | bytes 12649472 | tf_op jit(solution)/shard_map/convert_element_type | solution.py:55
  96.0 10.4 %convolution_convert_fusion = bf16[8192,1024]{1,0:T(8,128)(2,1)} fusion(bf16[8192,256]{1,0:T(8,128)(2,1)} %bitcast.110, bf16[256,1024]{1,0:T(8,128)(2,1)S(1)} %bitcast.114), kind=kOutput, calls=%fused_computation.16 | convolution fusion | flops 4303355904 | bytes 21495808 | tf_op jit(solution)/shard_map/dot_general | solution.py:56
  106.4 20.7 %copy.73 = bf16[8192,1024]{0,1:T(8,128)(2,1)} copy(bf16[8192,1024]{1,0:T(8,128)(2,1)} %convolution_convert_fusion) | data formatting | bytes 33554432 | tf_op jit(solution)/shard_map/convert_element_type | solution.py:58
  127.2 12.1 %copy.99 = bf16[128,8,16,512]{3,2,1,0:T(8,128)(2,1)S(1)} copy(bf16[128,8,16,512]{3,1,2,0:T(8,128)(2,1)} %bitcast.105) | data formatting | bytes 33554432
  139.3 20.6 %copy.74 = bf16[16,512,4,8,32]{1,4,3,2,0:T(8,128)(2,1)} copy(bf16[16,512,4,8,32]{1,0,4,3,2:T(8,128)(2,1)S(1)} %bitcast.106) | data formatting | bytes 33554432 | tf_op jit(solution)/shard_map/while | solution.py:101
  159.8 81.2 %while.10 = (s32[]{:T(128)}, bf16[16,512,256]{2,1,0:T(8,128)(2,1)}, bf16[16,512,4,8,32]{1,4,3,2,0:T(8,128)(2,1)}, s32[]{:T(128)}) while((s32[]{:T(128)}, bf16[16,512,256]{2,1,0:T(8,128)(2,1)}, bf16[16,512,4,8,32]{1,4,3,2,0:T(8,128)(2,1)}, s32[]{:T(128)}) %tuple.37), condition=%wide.region_4.0_spmd, body=%wide.region_2.4_spmd.sunk | while | flops 277737472 | bytes 21267000 | solution.py:101
  161.1 1.4 fusion.34
  162.6 1.5 fusion.35
  166.2 1.4 fusion.34
  167.7 1.5 fusion.35
  172.7 1.5 fusion.35
  177.8 1.5 fusion.35
  182.9 1.5 fusion.35
  188.0 1.5 fusion.35
  193.0 1.5 fusion.35
  198.1 1.5 fusion.35
  201.8 1.4 fusion.34
  203.2 1.5 fusion.35
  208.3 1.5 fusion.35
  213.4 1.5 fusion.35
  217.0 1.4 fusion.34
  218.4 1.5 fusion.35
  223.5 1.5 fusion.35
  228.6 1.5 fusion.35
  233.7 1.5 fusion.35
  237.3 1.4 fusion.34
  238.7 1.5 fusion.35
  241.1 5.9 %fusion.19 = bf16[8192,256]{1,0:T(8,128)(2,1)S(1)} fusion(f32[8192,256]{1,0:T(8,128)} %bitcast.107, bf16[8192,256]{1,0:T(8,128)(2,1)} %bitcast.112, bf16[256,256]{1,0:T(8,128)(2,1)S(1)} %copy-done), kind=kOutput, calls=%fused_computation.18 | convolution fusion | flops 1077936128 | bytes 16908288 | tf_op jit(solution)/shard_map/dot_general | solution.py:75
  247.0 2.4 copy.76
  249.4 1.6 slice_bitcast_fusion.7
  251.0 29.6 %all_to_all.22 = bf16[4,64,1,16,256]{4,3,1,2,0:T(8,128)(2,1)S(1)} all-to-all(bf16[4,64,1,16,256]{4,3,1,2,0:T(8,128)(2,1)S(1)} %get-tuple-element.67), channel_id=1, replica_groups=mesh['seq_0'=4,'seq_1'=4,'seq_2'=2,'res'=4] {'res'}, dimensions={0} | all-to-all | bytes 4194304 | tf_op jit(solution)/shard_map/all_to_all | solution.py:38
  280.6 4.7 %all-to-all-start.2 = ((bf16[4,64,1,16,256]{4,3,1,2,0:T(8,128)(2,1)}), bf16[4,64,1,16,256]{4,3,1,2,0:T(8,128)(2,1)}, u32[]{:S(2)}, u32[]{:S(2)}) async-start(bf16[4,64,1,16,256]{4,3,1,2,0:T(8,128)(2,1)} %get-tuple-element.68), calls=%async_computation.2 | async-start | bytes 4194304 | tf_op jit(solution)/shard_map/all_to_all | solution.py:38
  285.8 23.9 %all-to-all-done.2 = bf16[4,64,1,16,256]{4,3,1,2,0:T(8,128)(2,1)} async-done(((bf16[4,64,1,16,256]{4,3,1,2,0:T(8,128)(2,1)}), bf16[4,64,1,16,256]{4,3,1,2,0:T(8,128)(2,1)}, u32[]{:S(2)}, u32[]{:S(2)}) %all-to-all-start.2) | async-done | bytes 2097184 | tf_op jit(solution)/shard_map/all_to_all | solution.py:38
  309.7 3.7 fusion.23
  313.8 4.2 %multiply_reduce_fusion = f32[128,4,16]{2,1,0:T(4,128)S(1)} fusion(f32[128,4,16]{2,1,0:T(4,128)S(1)} %copy.83, bf16[4,64,1,16,256]{4,3,1,2,0:T(8,128)(2,1)} %all-to-all-done.2, bf16[4,64,1,16,256]{4,3,1,2,0:T(8,128)(2,1)S(1)} %all_to_all.22), kind=kLoop, calls=%fused_computation.26 | loop fusion | flops 10477568 | bytes 4259840 | tf_op jit(solution)/shard_map/reduce_sum | solution.py:49
  318.5 4.0 %bitcast_convert_fusion.1 = (f32[128,4,1,16,256]{4,3,1,0,2:T(8,128)S(1)}, bf16[128,4,16,256]{3,2,1,0:T(8,128)(2,1)}) fusion(bf16[4,64,1,16,256]{4,3,1,2,0:T(8,128)(2,1)} %all-to-all-done.2, bf16[4,64,1,16,256]{4,3,1,2,0:T(8,128)(2,1)S(1)} %all_to_all.22), kind=kLoop, calls=%fused_computation.31 | loop fusion | flops 4194304 | bytes 16777216 | tf_op jit(solution)/shard_map/convert_element_type | solution.py:107
  322.4 4.5 %fusion.22 = bf16[8192,256]{1,0:T(8,128)(2,1)S(1)} fusion(f32[128,4,1,16,256]{4,3,1,0,2:T(8,128)S(1)} %get-tuple-element.65, f32[256]{0:T(256)S(1)} %copy-done.5, f32[8192]{0:T(1024)S(1)} %rsqrt.21, f32[8192]{0:T(1024)S(1)} %div.34), kind=kLoop, calls=%fused_computation.23 | loop fusion | flops 8388608 | bytes 12649472 | tf_op jit(solution)/shard_map/convert_element_type | solution.py:107
  329.2 6.9 %all-reduce.2 = (f32[]{:T(128)}, f32[]{:T(128)}) all-reduce(f32[]{:T(128)} %get-tuple-element.48, f32[]{:T(128)} %get-tuple-element.47), channel_id=1, replica_groups=mesh['seq_0'=4,'seq_1'=4,'seq_2'=2,'res'=4] {'seq_0'}, use_global_device_ids=true, to_apply=%region_10.11 | all-reduce | flops 2 | bytes 16 | tf_op jit(solution)/shard_map/psum | solution.py:43
  336.2 10.8 %all-reduce.1 = (f32[]{:T(128)}, f32[]{:T(128)}) all-reduce(f32[]{:T(128)} %get-tuple-element.59, f32[]{:T(128)} %get-tuple-element.60), channel_id=1, replica_groups=mesh['seq_0'=4,'seq_1'=4,'seq_2'=2,'res'=4] {'seq_1'}, use_global_device_ids=true, to_apply=%region_11.12 | all-reduce | flops 2 | bytes 16 | tf_op jit(solution)/shard_map/psum | solution.py:43
  346.9 7.9 %all-reduce.3 = (f32[]{:T(128)}, f32[]{:T(128)}) all-reduce(f32[]{:T(128)} %get-tuple-element.57, f32[]{:T(128)} %get-tuple-element.58), channel_id=1, replica_groups=mesh['seq_0'=4,'seq_1'=4,'seq_2'=2,'res'=4] {'seq_2'}, use_global_device_ids=true, to_apply=%region_12.13 | all-reduce | flops 2 | bytes 16 | tf_op jit(solution)/shard_map/psum | solution.py:43
  354.9 7.5 %all-reduce = (f32[]{:T(128)}, f32[]{:T(128)}) all-reduce(f32[]{:T(128)} %get-tuple-element.61, f32[]{:T(128)} %get-tuple-element.62), channel_id=1, replica_groups=mesh['seq_0'=4,'seq_1'=4,'seq_2'=2,'res'=4] {'res'}, use_global_device_ids=true, to_apply=%region_13.14 | all-reduce | flops 2 | bytes 16 | tf_op jit(solution)/shard_map/psum | solution.py:43
  (92 shorter events, 54.0 us)
Async XLA Ops:
  0.6 240.4 %copy-start = (bf16[256,256]{1,0:T(8,128)(2,1)S(1)}, bf16[256,256]{1,0:T(8,128)(2,1)}, u32[]{:S(2)}) copy-start(bf16[256,256]{1,0:T(8,128)(2,1)} %param.13) | copy-start | bytes 393220
  5.4 9.6 %copy-start.1 = (bf16[256,4,256]{2,1,0:T(4,128)(2,1)S(1)}, bf16[256,4,256]{2,1,0:T(4,128)(2,1)}, u32[]{:S(2)}) copy-start(bf16[256,4,256]{2,1,0:T(4,128)(2,1)} %param.12) | copy-start | bytes 1572868
  5.4 61.7 %all-to-all-start = ((bf16[16,32,16,256]{3,2,0,1:T(8,128)(2,1)}), bf16[16,32,16,256]{3,2,0,1:T(8,128)(2,1)}, u32[]{:S(2)}, u32[]{:S(2)}) async-start(bf16[16,32,16,256]{3,2,0,1:T(8,128)(2,1)} %copy.71), calls=%async_computation | async-start | bytes 8388608 | tf_op jit(solution)/shard_map/all_to_all | solution.py:87
  83.1 6.5 %copy-start.4 = (f32[256]{0:T(256)S(1)}, f32[256]{0:T(256)}, u32[]{:S(2)}) copy-start(f32[256]{0:T(256)} %param.11) | copy-start | bytes 3076
  251.0 34.3 %copy-start.2 = (s32[128,4,16]{0,2,1:T(8,128)S(1)}, s32[128,4,16]{0,2,1:T(8,128)}, u32[]{:S(2)}) copy-start(s32[128,4,16]{0,2,1:T(8,128)} %param.17) | copy-start | bytes 98308
  251.0 34.6 %copy-start.3 = (s32[128,4,16]{0,2,1:T(8,128)S(1)}, s32[128,4,16]{0,2,1:T(8,128)}, u32[]{:S(2)}) copy-start(s32[128,4,16]{0,2,1:T(8,128)} %param.16) | copy-start | bytes 98308
  280.6 29.1 %all-to-all-start.2 = ((bf16[4,64,1,16,256]{4,3,1,2,0:T(8,128)(2,1)}), bf16[4,64,1,16,256]{4,3,1,2,0:T(8,128)(2,1)}, u32[]{:S(2)}, u32[]{:S(2)}) async-start(bf16[4,64,1,16,256]{4,3,1,2,0:T(8,128)(2,1)} %get-tuple-element.68), calls=%async_computation.2 | async-start | bytes 4194304 | tf_op jit(solution)/shard_map/all_to_all | solution.py:38
  318.5 4.0 %copy-start.5 = (f32[256]{0:T(256)S(1)}, f32[256]{0:T(256)}, u32[]{:S(2)}) copy-start(f32[256]{0:T(256)} %param.14) | copy-start | bytes 3076
  322.4 4.5 %copy-start.6 = (bf16[256,23]{0,1:T(8,128)(2,1)S(1)}, bf16[256,23]{0,1:T(8,128)(2,1)}, u32[]{:S(2)}) copy-start(bf16[256,23]{0,1:T(8,128)(2,1)} %param.15) | copy-start | bytes 35332
where the time goes:
time: 370 us; the launch traced here: 367 us
  local copies, waits for them, and re-layouts  106 us (29%)
  waiting for transfers between devices  75.9 us (21%)
  matrix products  64 us (17%)
  blocking collectives  62.7 us (17%)
  other arithmetic  37.8 us (10%)
  starting transfers between devices  14.3 us (4%)
  between operations  5.06 us (1%)
    all_to_all x1, waiting for transfers between devices, on_device(): lax.all_to_all(split_view, SEQ, split_axis=1, concat_axis=0, tiled=True)  52 us
    psum x4, blocking collectives, over_axes(): return functools.reduce(lax.psum, axes, array)  33.1 us
    all_to_all x1, blocking collectives, exchange_in_pieces(): lax.all_to_all(piece, axis, split_axis=0, concat_axis=0, tiled=True)  29.6 us
    all_to_all x1, waiting for transfers between devices, exchange_in_pieces(): lax.all_to_all(piece, axis, split_axis=0, concat_axis=0, tiled=True)  23.9 us
    dot_general x16, matrix products, column_attention(): jnp.einsum('hst,thd->shd', probs.astype(jnp.bfloat16), value_part, prefer...  23.4 us
    dot_general x16, matrix products, column_attention(): jnp.einsum('shd,thd->hst', queries, key_part, preferred_element_type=jnp....  23 us
    convert_element_type x1, local copies, waits for them, and re-layouts, project(): return jnp.dot(normed, w_proj.reshape(features, 4 * features), preferred_...  20.7 us
    squeeze x16, local copies, waits for them, and re-layouts, on_device(): lax.map(per_column, projected).reshape(col_count * seq_total, features)  20.7 us
  transfers between devices with their start and end apart: 2, of which 2 were waited for; matrix products, arithmetic and copies ran while one was open for 0% of the time, Pallas kernels for 0%

commit v1 on v0

v1 whole, which is shorter than its diff:
```python
import functools
import math

import jax
import jax.numpy as jnp
from jax import lax
from jax.experimental import pallas as pl
from jax.experimental.pallas import tpu as pltpu
from jax.sharding import Mesh
from jax.sharding import PartitionSpec as P

HEADS = 8
HEAD_DIM = 32
CLASSES = 23
C = 256
NSEQ = 32
NRES = 4
ROWS = 16
S = 512
COLS = 16
CHUNK = 2
CHUNKS = COLS // CHUNK
VAUG = 48
LPAD = 32
AXES = ("seq_0", "seq_1", "seq_2", "res")
SEQ = AXES[:3]
MESH = pl.DeviceIdType.MESH
BF = jnp.bfloat16
F32 = jnp.float32
QSCALE = HEAD_DIM ** (-0.5) * math.log2(math.e)


def seq_coords(index):
    return index // 8, (index // 2) % 4, index % 2


def swap_matrix(outer, inner):
    n = outer * inner
    row = lax.broadcasted_iota(jnp.int32, (n, n), 0)
    col = lax.broadcasted_iota(jnp.int32, (n, n), 1)
    source = (row % outer) * inner + row // outer
    return jnp.where(col == source, 1.0, 0.0).astype(BF)


def normed_rows(values, gain):
    mean = jnp.mean(values, axis=-1, keepdims=True)
    centred = values - mean
    spread = jnp.mean(centred * centred, axis=-1, keepdims=True)
    return (centred * lax.rsqrt(spread + 1e-05) * gain).astype(BF)


def dot(a, b, dims=((1,), (0,))):
    return lax.dot_general(a, b, (dims, ((), ())), preferred_element_type=F32)


def exchange_kernel(
    align_hbm, codes_ref, gain_attn, w_k, w_qvg, w_out, gain_head, w_head,
    out_hbm, stats_ref,
    align_v, sendbuf, recv, outbuf, codes_r, qz, va, gt, gated_t, k_nat, perm, acc, st_y, st_s,
    load_sem, send_sem, recv_sem, ysend_sem, yrecv_sem, own_sem, code_sem, csend_sem, ar_sem, ars_sem,
):
    x, z, core, y = (lax.axis_index(a) for a in AXES)
    me = (x * 4 + z) * 2 + core

    def seq_device(i):
        dx, dz, dc = seq_coords(lax.rem(me + i, NSEQ))
        return (dx, dz, dc, y)

    def res_device(k):
        return (x, z, core, lax.rem(y + k, NRES))

    loads = [
        pltpu.make_async_copy(
            align_hbm.at[:, 0, pl.ds(128 * j, 128)], align_v.at[:, pl.ds(128 * j, 128)], load_sem.at[j]
        )
        for j in range(4)
    ]
    for load in loads:
        load.start()

    barrier = pltpu.get_barrier_semaphore()

    @pl.loop(1, NSEQ)
    def _(i):
        pl.semaphore_signal(barrier, inc=1, device_id=seq_device(i), device_id_type=MESH)

    for k in range(1, NRES):
        pl.semaphore_signal(barrier, inc=1, device_id=res_device(k), device_id_type=MESH)

    perm[...] = swap_matrix(ROWS, COLS)
    qz[...] = jnp.zeros_like(qz)
    va[...] = jnp.ones_like(va)
    acc[...] = jnp.zeros_like(acc)
    for j in range(4):
        loads[j].wait()

        @pl.loop(8 * j, 8 * j + 8)
        def _(d):
            block = align_v[:, pl.ds(pl.multiple_of(d * COLS, COLS), COLS)].reshape(ROWS * COLS, C)
            moved = dot(perm[...], block).astype(BF)
            sendbuf[d] = moved.reshape(COLS, ROWS, C)

    for m in range(CHUNKS):
        recv[m, me] = sendbuf[me, pl.ds(CHUNK * m, CHUNK)]
    codes_r[y] = codes_ref[y]

    pl.semaphore_wait(barrier, NSEQ - 1 + NRES - 1)

    for k in range(1, NRES):
        pltpu.make_async_remote_copy(
            codes_ref.at[lax.rem(y + k, NRES)], codes_r.at[y], csend_sem, code_sem,
            device_id=res_device(k), device_id_type=MESH,
        ).start()

    @pl.loop(0, CHUNKS)
    def _(m):
        @pl.loop(1, NSEQ)
        def _(i):
            pltpu.make_async_remote_copy(
                sendbuf.at[lax.rem(me + i, NSEQ), pl.ds(m * CHUNK, CHUNK)], recv.at[m, me],
                send_sem, recv_sem.at[m], device_id=seq_device(i), device_id_type=MESH,
            ).start()

    pltpu.make_async_copy(codes_r.at[pl.ds(0, 3)], codes_r.at[pl.ds(0, 3)], code_sem).wait()
    count = jnp.sum((codes_r[...] >= 32).astype(F32), axis=0)
    acc[pl.ds(8, 8)] = count[:8] + count[8:]

    @pl.loop(0, COLS)
    def _(c):
        m = c // CHUNK
        j = c % CHUNK

        @pl.when(j == 0)
        def _():
            span = recv.at[m, pl.ds(0, NSEQ - 1)]
            pltpu.make_async_copy(span, span, recv_sem.at[m]).wait()

        rows = recv[m, :, j].reshape(S, C).astype(F32)
        normed = normed_rows(rows, gain_attn[...])
        k_nat[...] = dot(normed, w_k[...]).astype(BF)
        q_t = dot(w_qvg[pl.ds(0, C)], normed, ((1,), (1,)))
        q_t = (q_t * QSCALE).astype(BF)
        v_t = dot(w_qvg[pl.ds(C, C)], normed, ((1,), (1,))).astype(BF)
        for h in range(HEADS):
            part = slice(HEAD_DIM * h, HEAD_DIM * (h + 1))
            qz[h, part] = q_t[part]
            va[h, :HEAD_DIM] = v_t[part]
        gt[...] = dot(w_qvg[pl.ds(2 * C, C)], normed, ((1,), (1,))).astype(BF)

        @pl.loop(0, HEADS)
        def _(h):
            scores = dot(k_nat[...], qz[h])
            probs = jnp.exp2(scores).astype(BF)
            weighted = dot(va[h], probs)
            span = pl.ds(pl.multiple_of(h * HEAD_DIM, HEAD_DIM), HEAD_DIM)
            gate = jax.nn.sigmoid(gt[span].astype(F32))
            gated = weighted[:HEAD_DIM] / weighted[HEAD_DIM : HEAD_DIM + 1] * gate
            gated_t[span] = gated.astype(BF)

        added = dot(gated_t[...], w_out[...], ((0,), (0,)))
        updated = (recv[m, :, j].reshape(S, C).astype(F32) + added).astype(BF)
        outbuf[c] = updated

        for k in range(1, NRES):
            dst = lax.rem(y + k, NRES)
            pltpu.make_async_remote_copy(
                outbuf.at[c, pl.ds(pl.multiple_of(dst * 128, 128), 128)], out_hbm.at[y, c],
                ysend_sem, yrecv_sem, device_id=res_device(k), device_id_type=MESH,
            ).start()
        pltpu.make_async_copy(
            outbuf.at[c, pl.ds(pl.multiple_of(y * 128, 128), 128)], out_hbm.at[y, c], own_sem
        ).start()

        head_in = normed_rows(updated.astype(F32), gain_head[...])
        logits = dot(w_head[...], head_in, ((1,), (1,)))
        log_total = jnp.log(jnp.sum(jnp.exp(logits[:CLASSES]), axis=0, keepdims=True))
        classes = lax.broadcasted_iota(jnp.int32, (LPAD, 128), 0)
        for i in range(NRES):
            lanes = slice(128 * i, 128 * (i + 1))
            code = codes_r[i, pl.ds(c, 1)]
            picked = jnp.sum(
                jnp.where(classes == (code & 31), logits[:, lanes], 0.0), axis=0, keepdims=True
            )
            error = log_total[:, lanes] - picked
            acc[pl.ds(0, 1)] += jnp.where(code >= 32, error, 0.0)

    total_count = jnp.sum(acc[pl.ds(8, 8)], axis=0, keepdims=True)
    first = lax.broadcasted_iota(jnp.int32, (8, 128), 0) == 0
    st_y[y] = jnp.where(first, acc[pl.ds(0, 1)], total_count)
    for k in range(1, NRES):
        pltpu.make_async_remote_copy(
            st_y.at[y], st_y.at[y], ars_sem.at[0], ar_sem.at[0],
            device_id=res_device(k), device_id_type=MESH,
        ).start()
    pltpu.make_async_copy(st_y.at[pl.ds(0, 3)], st_y.at[pl.ds(0, 3)], ar_sem.at[0]).wait()
    st_s[me] = (st_y[0] + st_y[1]) + (st_y[2] + st_y[3])

    @pl.loop(1, NSEQ)
    def _(i):
        pltpu.make_async_remote_copy(
            st_s.at[me], st_s.at[me], ars_sem.at[1], ar_sem.at[1],
            device_id=seq_device(i), device_id_type=MESH,
        ).start()

    pltpu.make_async_copy(st_s.at[pl.ds(0, NSEQ - 1)], st_s.at[pl.ds(0, NSEQ - 1)], ar_sem.at[1]).wait()
    sums = jnp.sum(jnp.sum(st_s[...], axis=0), axis=1, keepdims=True)
    stats_ref[...] = jnp.broadcast_to(sums, (8, 128))

    pltpu.make_async_copy(st_y.at[pl.ds(0, 3)], st_y.at[pl.ds(0, 3)], ars_sem.at[0]).wait()
    pltpu.make_async_copy(st_s.at[pl.ds(0, NSEQ - 1)], st_s.at[pl.ds(0, NSEQ - 1)], ars_sem.at[1]).wait()
    pltpu.make_async_copy(codes_r.at[pl.ds(0, 3)], codes_r.at[pl.ds(0, 3)], csend_sem).wait()
    sent = sendbuf.at[pl.ds(0, NSEQ - 1)]
    pltpu.make_async_copy(sent, sent, send_sem).wait()
    pltpu.make_async_copy(out_hbm.at[0], out_hbm.at[0], own_sem).wait()
    three = out_hbm.at[pl.ds(0, 3)]
    pltpu.make_async_copy(three, three, ysend_sem).wait()
    pltpu.make_async_copy(three, three, yrecv_sem).wait()


def finish_kernel(part_ref, stats_ref, out_ref, loss_ref, share_ref):
    perm = swap_matrix(COLS, ROWS)
    for b in range(NRES):
        block = part_ref[b].reshape(COLS * ROWS, C)
        out_ref[:, b] = dot(perm, block).astype(BF).reshape(ROWS, COLS, C)
    loss_sum = stats_ref[0, 0]
    mask_count = stats_ref[1, 0]
    loss_ref[0, 0] = loss_sum / (1.0 + mask_count)
    share_ref[0, 0] = mask_count * (1.0 / 1048576)


def on_device(alignment, gain_attn, w_proj, w_out, gain_head, w_head, masked, labels):
    codes = jnp.transpose(labels + 32 * masked, (1, 2, 0))
    w_k = w_proj[:, 1]
    w_qvg = jnp.concatenate([w_proj[:, i].T for i in (0, 2, 3)], axis=0)
    w_head_t = jnp.pad(w_head.T, ((0, LPAD - CLASSES), (0, 0)))
    vmem = pl.BlockSpec(memory_space=pltpu.VMEM)
    hbm = pl.BlockSpec(memory_space=pl.ANY)
    dma = pltpu.SemaphoreType.DMA
    parts, stats = pl.pallas_call(
        exchange_kernel,
        out_shape=(
            jax.ShapeDtypeStruct((NRES, COLS, 128, C), BF),
            jax.ShapeDtypeStruct((8, 128), F32),
        ),
        in_specs=[hbm] + [vmem] * 7,
        out_specs=(hbm, vmem),
        scratch_shapes=[
            pltpu.VMEM((ROWS, S, C), BF),
            pltpu.VMEM((NSEQ, COLS, ROWS, C), BF),
            pltpu.VMEM((CHUNKS, NSEQ, CHUNK, ROWS, C), BF),
            pltpu.VMEM((COLS, S, C), BF),
            pltpu.VMEM((NRES, COLS, 128), jnp.int32),
            pltpu.VMEM((HEADS, C, S), BF),
            pltpu.VMEM((HEADS, VAUG, S), BF),
            pltpu.VMEM((C, S), BF),
            pltpu.VMEM((C, S), BF),
            pltpu.VMEM((S, C), BF),
            pltpu.VMEM((C, C), BF),
            pltpu.VMEM((16, 128), F32),
            pltpu.VMEM((NRES, 8, 128), F32),
            pltpu.VMEM((NSEQ, 8, 128), F32),
            dma((4,)), dma, dma((CHUNKS,)), dma, dma, dma, dma, dma, dma((2,)), dma((2,)),
        ],
        compiler_params=pltpu.CompilerParams(
            collective_id=0, has_side_effects=True, vmem_limit_bytes=60 * 2**20
        ),
        name="exchange",
    )(
        alignment, codes, gain_attn.reshape(1, C), w_k, w_qvg, w_out, gain_head.reshape(1, C), w_head_t,
    )
    smem = pl.BlockSpec(memory_space=pltpu.SMEM)
    updated, loss, share = pl.pallas_call(
        finish_kernel,
        grid=(128 // ROWS,),
        out_shape=(
            jax.ShapeDtypeStruct((128, NRES, COLS, C), BF),
            jax.ShapeDtypeStruct((1, 1), F32),
            jax.ShapeDtypeStruct((1, 1), F32),
        ),
        in_specs=[pl.BlockSpec((NRES, COLS, ROWS, C), lambda r: (0, 0, r, 0)), smem],
        out_specs=(pl.BlockSpec((ROWS, NRES, COLS, C), lambda r: (r, 0, 0, 0)), smem, smem),
        name="finish",
    )(parts, stats)
    return updated, loss.reshape(()), share.reshape(())


def solution(mesh):
    split = Mesh(mesh.devices.reshape(4, 4, 2, mesh.shape["res"]), AXES)
    return jax.shard_map(
        on_device,
        mesh=split,
        in_specs=(
            P(SEQ, "res", None, None), P(), P(), P(), P(), P(),
            P("res", None, SEQ), P("res", None, SEQ),
        ),
        out_specs=(P("res", None, SEQ, None), P(), P()),
        check_vma=False,
    )
```

time: 370 us -> 133 us (0.36)
  Pallas kernels: 0 us -> 125 us
  local copies, waits for them, and re-layouts: 106 us -> 5.33 us
  waiting for transfers between devices: 75.9 us -> 0 us
  matrix products: 64 us -> 0 us
  blocking collectives: 62.7 us -> 0 us
  other arithmetic: 37.8 us -> 2.16 us
  starting transfers between devices: 14.3 us -> 0 us
  between operations: 5.06 us -> 0.65 us
    pallas_call x0 -> x2, Pallas kernels: none -> 125 us  [the longest x1 117 us: on_device(): pl.pallas_call(exchange_kernel, out_shape=(jax.ShapeDtypeStruct((NRES, CO...]
    all_to_all x2 -> x0, waiting for transfers between devices: 75.9 us -> none  [the longest x1 52 us: on_device(): lax.all_to_all(split_view, SEQ, split_axis=1, concat_axis=0, tiled=True)]
    dot_general x35 -> x0, matrix products: 64 us -> none  [the longest x16 23.4 us: column_attention(): jnp.einsum('hst,thd->shd', probs.astype(jnp.bfloat16), value_part, prefer...]
    psum x4 -> x0, blocking collectives: 33.1 us -> none  [over_axes(): return functools.reduce(lax.psum, axes, array)]
    all_to_all x1 -> x0, blocking collectives: 29.6 us -> none  [exchange_in_pieces(): lax.all_to_all(piece, axis, split_axis=0, concat_axis=0, tiled=True)]
    convert_element_type x2 -> x0, local copies, waits for them, and re-layouts: 28.8 us -> none  [the longest x1 20.7 us: project(): return jnp.dot(normed, w_proj.reshape(features, 4 * features), preferred_...]
    squeeze x16 -> x0, local copies, waits for them, and re-layouts: 20.7 us -> none  [on_device(): lax.map(per_column, projected).reshape(col_count * seq_total, features)]
    while x1 -> x0, local copies, waits for them, and re-layouts: 20.6 us -> none  [on_device(): lax.map(per_column, projected).reshape(col_count * seq_total, features)]
  transfers between devices with their start and end apart: 2 -> 0, of which waited for: 2 -> 0; matrix products, arithmetic and copies ran while one was open for 0% -> 0% of each run, Pallas kernels for 0% -> 0%
where the time goes in v1:
time: 133 us
  Pallas kernels  125 us (94%)
  local copies, waits for them, and re-layouts  5.33 us (4%)
  other arithmetic  2.16 us (2%)
    pallas_call x1, Pallas kernels, on_device(): pl.pallas_call(exchange_kernel, out_shape=(jax.ShapeDtypeStruct((NRES, CO...  117 us
    pallas_call x1, Pallas kernels, on_device(): pl.pallas_call(finish_kernel, grid=(128 // ROWS,), out_shape=(jax.ShapeDt...  7.58 us
    slice x1, local copies, waits for them, and re-layouts, on_device(): w_qvg = jnp.concatenate([w_proj[:, i].T for i in (0, 2, 3)], axis=0)  2.93 us

profile of v1, /device:TPU:1, one launch (start us, length us, event | category | flops | bytes accessed | tf_op | source)
XLA Modules:
  0.0 132.8 jit_solution(11591607046675429826)
XLA Ops:
  0.6 1.3 pad.4.w_head
  1.9 1.4 %add_bitcast_fusion.codes_ref = s32[4,16,128]{2,1,0:T(8,128)} fusion(s32[128,4,16]{0,2,1:T(8,128)} %param.15, s32[128,4,16]{0,2,1:T(8,128)} %param.14), kind=kLoop, calls=%fused_computation.2 | loop fusion | flops 16384 | bytes 98304 | tf_op jit(solution)/shard_map/transpose | solution.py:232
  3.3 2.9 %fusion = (bf16[256,1,256]{2,1,0:T(2,128)(2,1)S(1)}, bf16[256,1,256]{2,1,0:T(2,128)(2,1)S(1)}, bf16[256,1,256]{2,1,0:T(2,128)(2,1)S(1)}, bf16[256,1,256]{2,1,0:T(2,128)(2,1)S(1)}) fusion(bf16[256,4,256]{2,1,0:T(4,128)(2,1)} %param.10), kind=kLoop, calls=%fused_computation.3 | loop fusion | bytes 1048576 | tf_op jit(solution)/shard_map/slice | solution.py:234
  6.3 0.1 copy.16
  6.4 0.7 copy.20
  7.1 0.1 copy.17
  7.2 0.1 copy.18
  7.4 0.8 pad_maximum_fusion.w_qvg
  8.1 117.1 %exchange.1 = (bf16[4,16,128,256]{3,2,1,0:T(8,128)(2,1)}, f32[8,128]{1,0:T(8,128)}) custom-call(bf16[16,1,512,256]{3,2,1,0:T(8,128)(2,1)} %align_hbm.1, s32[4,16,128]{2,1,0:T(8,128)} %add_bitcast_fusion.codes_ref, f32[1,256]{1,0:T(1,128)} %bitcast.24, bf16[256,256]{1,0:T(8,128)(2,1)} %bitcast.19, bf16[768,256]{1,0:T(8,128)(2,1)} %pad_maximum_fusion.w_qvg, ...), custom_call_target="tpu_custom_call" | custom-call | tf_op jit(solution)/shard_map/exchange/pallas_call | solution.py:239
  125.2 7.6 %finish.1 = (bf16[128,4,16,256]{3,2,1,0:T(8,128)(2,1)}, f32[1,1]{1,0:T(1,128)}, f32[1,1]{1,0:T(1,128)}) custom-call(bf16[4,16,128,256]{3,2,1,0:T(8,128)(2,1)} %get-tuple-element.8.part_ref, f32[8,128]{1,0:T(8,128)} %get-tuple-element.9.stats_ref), custom_call_target="tpu_custom_call" | custom-call | tf_op jit(solution)/shard_map/finish/pallas_call | solution.py:272

commit v2 on v1

v2 whole, which is shorter than its diff:
```python
import math

import jax
import jax.numpy as jnp
from jax import lax
from jax.experimental import pallas as pl
from jax.experimental.pallas import tpu as pltpu
from jax.sharding import Mesh
from jax.sharding import PartitionSpec as P

HEADS = 8
HEAD_DIM = 32
CLASSES = 23
C = 256
NSEQ = 32
NRES = 4
ROWS = 16
S = 512
COLS = 16
VAUG = 48
LPAD = 32
VMEM_LIMIT = 48 * 2**20
AXES = ("seq_0", "seq_1", "seq_2", "res")
SEQ = AXES[:3]
MESH = pl.DeviceIdType.MESH
BF = jnp.bfloat16
F32 = jnp.float32
QSCALE = HEAD_DIM ** (-0.5) * math.log2(math.e)


def normed_rows(values, gain):
    mean = jnp.mean(values, axis=-1, keepdims=True)
    centred = values - mean
    spread = jnp.mean(centred * centred, axis=-1, keepdims=True)
    return (centred * lax.rsqrt(spread + 1e-05) * gain).astype(BF)


def dot(a, b, dims=((1,), (0,))):
    return lax.dot_general(a, b, (dims, ((), ())), preferred_element_type=F32)


def exchange_kernel(
    align_hbm, w_proj_hbm, w_out_ref, w_head_hbm, gains_a_hbm, gains_h_hbm, masked_hbm, labels_hbm,
    out_ref, stats_ref,
    align_v, sendbuf, recv, outbuf, codes, codes_r, w_proj_v, w_k, w_qvg, w_out, w_head_v, w_head,
    gain_attn, gain_head, masked_v, labels_v, qz, va, sg, gated_t, k_nat, sb, nm, hi, acc, st_y, st_s,
    load_sem, small_sem, send_sem, recv_sem, ysend_sem, yrecv_sem, code_sem, csend_sem, ar_sem, ars_sem,
):
    x, z, core, y = (lax.axis_index(a) for a in AXES)
    me = (x * 4 + z) * 2 + core

    at_x = [lax.rem(x + d, 4) for d in range(4)]
    at_z = [lax.rem(z + d, 4) for d in range(4)]
    at_core = [core, 1 - core]
    at_y = [lax.rem(y + d, NRES) for d in range(NRES)]

    def seq_device(i):
        return (at_x[i // 8], at_z[i // 2 % 4], at_core[i % 2], y)

    def seq_index(i):
        return (at_x[i // 8] * 4 + at_z[i // 2 % 4]) * 2 + at_core[i % 2]

    def res_device(k):
        return (x, z, core, at_y[k])

    barrier = pltpu.get_barrier_semaphore()

    for i in range(1, NSEQ):
        pl.semaphore_signal(barrier, inc=1, device_id=seq_device(i), device_id_type=MESH)

    for k in range(1, NRES):
        pl.semaphore_signal(barrier, inc=1, device_id=res_device(k), device_id_type=MESH)

    loads = [
        pltpu.make_async_copy(
            align_hbm.at[:, 0, pl.ds(128 * j, 128)], align_v.at[:, pl.ds(128 * j, 128)], load_sem.at[j]
        )
        for j in range(4)
    ]
    small = [
        pltpu.make_async_copy(src, dst, small_sem.at[n])
        for n, (src, dst) in enumerate(
            (
                (masked_hbm, masked_v), (labels_hbm, labels_v), (w_proj_hbm, w_proj_v),
                (w_out_ref, w_out), (w_head_hbm, w_head_v),
                (gains_a_hbm, gain_attn), (gains_h_hbm, gain_head),
            )
        )
    ]
    for copy in loads + small:
        copy.start()

    for j in range(4):
        loads[j].wait()

        @pl.loop(0, 2)
        def _(g):
            for u in range(4):
                d = 8 * j + 4 * g + u
                block = align_v[:, pl.ds(pl.multiple_of(d * COLS, COLS), COLS)]
                sendbuf[d] = jnp.swapaxes(block, 0, 1)

    recv[:, me] = sendbuf[me]

    for copy in small:
        copy.wait()
    codes[...] = labels_v[...] + 32 * masked_v[...]
    codes_r[y] = codes[y]

    pl.semaphore_wait(barrier, NSEQ - 1 + NRES - 1)

    for k in range(1, NRES):
        pltpu.make_async_remote_copy(
            codes.at[lax.rem(y + k, NRES)], codes_r.at[y], csend_sem, code_sem,
            device_id=res_device(k), device_id_type=MESH,
        ).start()

    @pl.loop(0, COLS)
    def _(c):
        for i in range(1, NSEQ):
            pltpu.make_async_remote_copy(
                sendbuf.at[seq_index(i), c], recv.at[c, me],
                send_sem, recv_sem.at[c], device_id=seq_device(i), device_id_type=MESH,
            ).start()

    for n, i in enumerate((0, 2, 3)):
        w_qvg[pl.ds(C * n, C)] = w_proj_v[:, i].astype(F32).T.astype(BF)
    w_k[...] = w_proj_v[:, 1]
    w_head[...] = jnp.zeros_like(w_head)
    w_head[:CLASSES] = w_head_v[...]
    gated_t[...] = jnp.zeros_like(gated_t)
    acc[...] = jnp.zeros_like(acc)
    for p in range(2):
        qz[p] = jnp.zeros((HEADS, C, S), BF)
        va[p] = jnp.ones((HEADS, VAUG, S), BF)

    pltpu.make_async_copy(codes_r.at[pl.ds(0, 3)], codes_r.at[pl.ds(0, 3)], code_sem).wait()
    count = jnp.sum((codes_r[...] >= 32).astype(F32), axis=0)
    acc[pl.ds(8, 8)] = count[:8] + count[8:]

    def arrived(c):
        span = recv.at[c, pl.ds(0, NSEQ - 1)]
        pltpu.make_async_copy(span, span, recv_sem.at[c]).wait()

    def rows(c, start, n):
        return recv[c, pl.ds(start // ROWS, n // ROWS)].reshape(n, C).astype(F32)

    def before(c, p):
        def norm(start):
            def run():
                nm[pl.ds(start, 128)] = normed_rows(rows(c, start, 128), gain_attn[...])
            return run

        def keys():
            k_nat[p] = dot(nm[...], w_k[...]).astype(BF)

        def queries():
            q_t = (dot(w_qvg[pl.ds(0, C)], nm[...], ((1,), (1,))) * QSCALE).astype(BF)
            for h in range(HEADS):
                part = slice(HEAD_DIM * h, HEAD_DIM * (h + 1))
                qz[p, h, part] = q_t[part]

        def values():
            v_t = dot(w_qvg[pl.ds(C, C)], nm[...], ((1,), (1,))).astype(BF)
            for h in range(HEADS):
                va[p, h, :HEAD_DIM] = v_t[HEAD_DIM * h : HEAD_DIM * (h + 1)]

        def gates():
            g_t = dot(w_qvg[pl.ds(2 * C, C)], nm[...], ((1,), (1,))).astype(BF).astype(F32)
            sg[p] = 0.5 * jnp.tanh(0.5 * g_t) + 0.5

        return [norm(0), norm(128), norm(256), norm(384), keys, queries, values, gates]

    def after(c, p, live):
        def project(start):
            def run():
                added = dot(gated_t[p, :, start : start + 256], w_out[...], ((0,), (0,)))
                outbuf[c, pl.ds(start, 256)] = (rows(c, start, 256) + added).astype(BF)
            return run

        def norm(start):
            def run():
                hi[pl.ds(start, 256)] = normed_rows(outbuf[c, pl.ds(start, 256)].astype(F32), gain_head[...])
            return run

        def loss():
            logits = dot(w_head[...], hi[...], ((1,), (1,)))
            log_total = jnp.log(jnp.sum(jnp.exp(logits[:CLASSES]), axis=0, keepdims=True))
            classes = lax.broadcasted_iota(jnp.int32, (LPAD, 128), 0)
            total = jnp.zeros((1, 128), F32)
            for i in range(NRES):
                lanes = slice(128 * i, 128 * (i + 1))
                code = codes_r[i, pl.ds(c, 1)]
                picked = jnp.sum(
                    jnp.where(classes == (code & 31), logits[:, lanes], 0.0), axis=0, keepdims=True
                )
                total += jnp.where(code >= 32, log_total[:, lanes] - picked, 0.0)
            if live is not None:
                total = jnp.where(live, total, 0.0)
            acc[pl.ds(0, 1)] += total

        return [project(0), project(256), norm(0), norm(256), loss]

    def send_out(c):
        for k in range(1, NRES):
            dst = lax.rem(y + k, NRES)
            pltpu.make_async_remote_copy(
                outbuf.at[c, pl.ds(pl.multiple_of(dst * 128, 128), 128)], out_ref.at[y, c],
                ysend_sem, yrecv_sem, device_id=res_device(k), device_id_type=MESH,
            ).start()
        out_ref[y, c] = outbuf[c, pl.ds(pl.multiple_of(y * 128, 128), 128)]

    def score(p, h):
        sb[h % 2] = dot(k_nat[p], qz[p, h])

    def attend(p, h):
        weighted = dot(va[p, h], jnp.exp2(sb[h % 2]).astype(BF))
        part = slice(HEAD_DIM * h, HEAD_DIM * (h + 1))
        inverse = 1.0 / weighted[HEAD_DIM : HEAD_DIM + 1]
        gated_t[p, part] = (weighted[:HEAD_DIM] * inverse * sg[p, part]).astype(BF)

    def body(c, p, following, live):
        slots = [[] for _ in range(HEADS)]
        if following is not None:
            arrived(following)
            for slot, piece in enumerate(before(following, 1 - p)):
                slots[slot].append(piece)
        last = c - 1 if live is None else jnp.maximum(c - 1, 0)
        for slot, piece in zip((0, 1, 3, 4, 6), after(last, 1 - p, live)):
            slots[slot].append(piece)
        for h in range(HEADS):
            if h + 1 < HEADS:
                score(p, h + 1)
            for piece in slots[h]:
                piece()
            if h + 1 == HEADS and following is not None:
                score(1 - p, 0)
            attend(p, h)
        if live is None:
            send_out(last)
        else:
            @pl.when(live)
            def _():
                send_out(last)

    arrived(0)
    for piece in before(0, 0):
        piece()
    score(0, 0)

    @pl.loop(0, COLS // 2 - 1)
    def _(i):
        body(2 * i, 0, 2 * i + 1, i > 0)
        body(2 * i + 1, 1, 2 * i + 2, None)

    body(COLS - 2, 0, COLS - 1, None)
    body(COLS - 1, 1, None, None)
    final = after(COLS - 1, 1, None)
    final[0]()
    final[1]()
    send_out(COLS - 1)
    for piece in final[2:]:
        piece()

    total_count = jnp.sum(acc[pl.ds(8, 8)], axis=0, keepdims=True)
    first = lax.broadcasted_iota(jnp.int32, (8, 128), 0) == 0
    st_y[y] = jnp.where(first, acc[pl.ds(0, 1)], total_count)
    for k in range(1, NRES):
        pltpu.make_async_remote_copy(
            st_y.at[y], st_y.at[y], ars_sem.at[0], ar_sem.at[0],
            device_id=res_device(k), device_id_type=MESH,
        ).start()
    pltpu.make_async_copy(st_y.at[pl.ds(0, 3)], st_y.at[pl.ds(0, 3)], ar_sem.at[0]).wait()
    st_s[me] = (st_y[0] + st_y[1]) + (st_y[2] + st_y[3])

    for i in range(1, NSEQ):
        pltpu.make_async_remote_copy(
            st_s.at[me], st_s.at[me], ars_sem.at[1], ar_sem.at[1],
            device_id=seq_device(i), device_id_type=MESH,
        ).start()

    pltpu.make_async_copy(st_s.at[pl.ds(0, NSEQ - 1)], st_s.at[pl.ds(0, NSEQ - 1)], ar_sem.at[1]).wait()
    sums = jnp.sum(jnp.sum(st_s[...], axis=0), axis=1, keepdims=True)
    stats_ref[...] = jnp.broadcast_to(sums, (8, 128))

    pltpu.make_async_copy(st_y.at[pl.ds(0, 3)], st_y.at[pl.ds(0, 3)], ars_sem.at[0]).wait()
    pltpu.make_async_copy(st_s.at[pl.ds(0, NSEQ - 1)], st_s.at[pl.ds(0, NSEQ - 1)], ars_sem.at[1]).wait()
    pltpu.make_async_copy(codes_r.at[pl.ds(0, 3)], codes_r.at[pl.ds(0, 3)], csend_sem).wait()
    sent = sendbuf.at[pl.ds(0, NSEQ - 1)]
    pltpu.make_async_copy(sent, sent, send_sem).wait()
    three = out_ref.at[pl.ds(0, 3)]
    pltpu.make_async_copy(three, three, ysend_sem).wait()
    pltpu.make_async_copy(three, three, yrecv_sem).wait()


def finish_kernel(part_ref, stats_ref, out_hbm, loss_ref, share_ref, moved, sem):
    copies = []
    for g in range(128 // ROWS):
        span = pl.ds(ROWS * g, ROWS)
        for b in range(NRES):
            moved[span, b] = jnp.swapaxes(part_ref[b, :, span], 0, 1)
        copies.append(pltpu.make_async_copy(moved.at[span], out_hbm.at[span], sem.at[g]))
        copies[-1].start()
    loss_sum = stats_ref[0, 0]
    mask_count = stats_ref[1, 0]
    loss_ref[0, 0] = loss_sum / (1.0 + mask_count)
    share_ref[0, 0] = mask_count * (1.0 / 1048576)
    for copy in copies:
        copy.wait()


def on_device(alignment, gain_attn, w_proj, w_out, gain_head, w_head, masked, labels):
    vmem = pl.BlockSpec(memory_space=pltpu.VMEM)
    hbm = pl.BlockSpec(memory_space=pltpu.HBM)
    dma = pltpu.SemaphoreType.DMA
    parts, stats = pl.pallas_call(
        exchange_kernel,
        out_shape=(
            jax.ShapeDtypeStruct((NRES, COLS, 128, C), BF),
            jax.ShapeDtypeStruct((8, 128), F32),
        ),
        in_specs=[hbm] * 8,
        out_specs=(vmem, vmem),
        scratch_shapes=[
            pltpu.VMEM((ROWS, S, C), BF),
            pltpu.VMEM((NSEQ, COLS, ROWS, C), BF),
            pltpu.VMEM((COLS, NSEQ, ROWS, C), BF),
            pltpu.VMEM((COLS, S, C), BF),
            pltpu.VMEM((NRES, COLS, 128), jnp.int32),
            pltpu.VMEM((NRES, COLS, 128), jnp.int32),
            pltpu.VMEM((C, 4, C), BF),
            pltpu.VMEM((C, C), BF),
            pltpu.VMEM((3 * C, C), BF),
            pltpu.VMEM((C, C), BF),
            pltpu.VMEM((CLASSES, C), BF),
            pltpu.VMEM((LPAD, C), BF),
            pltpu.VMEM((1, C), F32),
            pltpu.VMEM((1, C), F32),
            pltpu.VMEM((NRES, COLS, 128), jnp.int32),
            pltpu.VMEM((NRES, COLS, 128), jnp.int32),
            pltpu.VMEM((2, HEADS, C, S), BF),
            pltpu.VMEM((2, HEADS, VAUG, S), BF),
            pltpu.VMEM((2, C, S), F32),
            pltpu.VMEM((2, C, S), BF),
            pltpu.VMEM((2, S, C), BF),
            pltpu.VMEM((2, S, S), F32),
            pltpu.VMEM((S, C), BF),
            pltpu.VMEM((S, C), BF),
            pltpu.VMEM((16, 128), F32),
            pltpu.VMEM((NRES, 8, 128), F32),
            pltpu.VMEM((NSEQ, 8, 128), F32),
            dma((4,)), dma((7,)), dma, dma((COLS,)), dma, dma, dma, dma, dma((2,)), dma((2,)),
        ],
        compiler_params=pltpu.CompilerParams(
            collective_id=0, has_side_effects=True, vmem_limit_bytes=VMEM_LIMIT
        ),
        name="exchange",
    )(
        alignment, w_proj, w_out, w_head.T, gain_attn.reshape(1, C), gain_head.reshape(1, C),
        jnp.transpose(masked, (1, 2, 0)), jnp.transpose(labels, (1, 2, 0)),
    )
    smem = pl.BlockSpec(memory_space=pltpu.SMEM)
    updated, loss, share = pl.pallas_call(
        finish_kernel,
        out_shape=(
            jax.ShapeDtypeStruct((128, NRES, COLS, C), BF),
            jax.ShapeDtypeStruct((1, 1), F32),
            jax.ShapeDtypeStruct((1, 1), F32),
        ),
        in_specs=[vmem, smem],
        out_specs=(hbm, smem, smem),
        scratch_shapes=[pltpu.VMEM((128, NRES, COLS, C), BF), dma((128 // ROWS,))],
        compiler_params=pltpu.CompilerParams(vmem_limit_bytes=16 * 2**20),
        name="finish",
    )(parts, stats)
    return updated, loss.reshape(()), share.reshape(())


def solution(mesh):
    split = Mesh(mesh.devices.reshape(4, 4, 2, mesh.shape["res"]), AXES)
    return jax.shard_map(
        on_device,
        mesh=split,
        in_specs=(
            P(SEQ, "res", None, None), P(), P(), P(), P(), P(),
            P("res", None, SEQ), P("res", None, SEQ),
        ),
        out_specs=(P("res", None, SEQ, None), P(), P()),
        check_vma=False,
    )
```

time: 133 us -> 87.5 us (0.66)
  Pallas kernels: 125 us -> 80.8 us
  other arithmetic: 2.16 us -> 0 us
    pallas_call x1, Pallas kernels: 117 us -> 77.5 us  [on_device(): pl.pallas_call(exchange_kernel, out_shape=(jax.ShapeDtypeStruct((NRES, CO...]
    unnamed x4 -> x14, local copies, waits for them, and re-layouts: 1.1 us -> 5.52 us
    pallas_call x1, Pallas kernels: 7.58 us -> 3.34 us  [on_device(): pl.pallas_call(finish_kernel, out_shape=(jax.ShapeDtypeStruct((128, NRES,...]
    slice x1 -> x0, local copies, waits for them, and re-layouts: 2.93 us -> none  [on_device(): w_qvg = jnp.concatenate([w_proj[:, i].T for i in (0, 2, 3)], axis=0)]
    transpose x1 -> x0, other arithmetic: 1.39 us -> none  [on_device(): codes = jnp.transpose(labels + 32 * masked, (1, 2, 0))]
where the time goes in v2:
time: 87.5 us; the launch traced here: 87.1 us
  Pallas kernels  80.8 us (92%)
  local copies, waits for them, and re-layouts  5.52 us (6%)
    pallas_call x1, Pallas kernels, on_device(): pl.pallas_call(exchange_kernel, out_shape=(jax.ShapeDtypeStruct((NRES, CO...  77.5 us
    unnamed x14, local copies, waits for them, and re-layouts  5.52 us
    pallas_call x1, Pallas kernels, on_device(): pl.pallas_call(finish_kernel, out_shape=(jax.ShapeDtypeStruct((128, NRES,...  3.34 us

profile of v2, /device:TPU:1, one launch (start us, length us, event | category | flops | bytes accessed | tf_op | source)
XLA Modules:
  0.0 87.1 jit_solution(2635957932650258001)
XLA Ops:
  0.6 0.0 copy-start
  0.6 1.0 %copy-done = bf16[256,4,256]{2,1,0:T(4,128)(2,1)S(1)} copy-done((bf16[256,4,256]{2,1,0:T(4,128)(2,1)S(1)}, bf16[256,4,256]{2,1,0:T(4,128)(2,1)}, u32[]{:S(2)}) %copy-start) | copy-done | bytes 524312
  1.7 0.0 copy-start.1
  1.7 0.9 %copy-done.1 = bf16[256,256]{1,0:T(8,128)(2,1)S(1)} copy-done((bf16[256,256]{1,0:T(8,128)(2,1)S(1)}, bf16[256,256]{1,0:T(8,128)(2,1)}, u32[]{:S(2)}) %copy-start.1) | copy-done | bytes 131096
  2.6 0.0 copy-start.2
  2.6 0.8 copy-done.2
  3.3 0.0 copy-start.3
  3.3 0.8 copy-done.3
  4.1 0.0 copy-start.4
  4.1 0.7 copy-done.4
  4.8 0.0 copy-start.5
  4.8 0.7 copy-done.5
  5.5 0.0 copy-start.6
  5.5 0.7 copy-done.6
  6.2 77.5 %exchange.1 = (bf16[4,16,128,256]{3,2,1,0:T(8,128)(2,1)S(1)}, f32[8,128]{1,0:T(8,128)S(1)}) custom-call(bf16[16,1,512,256]{3,2,1,0:T(8,128)(2,1)} %align_hbm.1, bf16[256,4,256]{2,1,0:T(4,128)(2,1)S(1)} %copy-done, bf16[256,256]{1,0:T(8,128)(2,1)S(1)} %copy-done.1, bf16[23,256]{1,0:T(8,128)(2,1)S(1)} %bitcast.9, f32[1,256]{1,0:T(1,128)S(1)} %bitcast.10, ...), custom_call_target="tpu_custom_call" | custom-call | tf_op jit(solution)/shard_map/exchange/pallas_call | solution.py:316
  83.6 3.3 %finish.1 = (bf16[128,4,16,256]{3,2,1,0:T(8,128)(2,1)}, f32[1,1]{1,0:T(1,128)}, f32[1,1]{1,0:T(1,128)}) custom-call(bf16[4,16,128,256]{3,2,1,0:T(8,128)(2,1)S(1)} %get-tuple-element.8.part_ref, f32[8,128]{1,0:T(8,128)S(1)} %get-tuple-element.9.stats_ref), custom_call_target="tpu_custom_call" | custom-call | tf_op jit(solution)/shard_map/finish/pallas_call | solution.py:363
Async XLA Ops:
  0.6 1.0 %copy-start = (bf16[256,4,256]{2,1,0:T(4,128)(2,1)S(1)}, bf16[256,4,256]{2,1,0:T(4,128)(2,1)}, u32[]{:S(2)}) copy-start(bf16[256,4,256]{2,1,0:T(4,128)(2,1)} %w_proj_hbm.1) | copy-start | bytes 1572868
  1.7 0.9 %copy-start.1 = (bf16[256,256]{1,0:T(8,128)(2,1)S(1)}, bf16[256,256]{1,0:T(8,128)(2,1)}, u32[]{:S(2)}) copy-start(bf16[256,256]{1,0:T(8,128)(2,1)} %w_out_ref.1) | copy-start | bytes 393220
  2.6 0.8 copy-start.2
  3.3 0.8 copy-start.3
  4.1 0.7 copy-start.4
  4.8 0.7 copy-start.5
  5.5 0.7 copy-start.6

commit v3 on v2

--- a/solution.py
+++ b/solution.py
@@ -19,7 +19,11 @@
 COLS = 16
 VAUG = 48
 LPAD = 32
-VMEM_LIMIT = 48 * 2**20
+AFTER_SLOTS = (0, 0, 1, 2, 3)
+BEFORE_SLOTS = (4, 4, 4, 4, 5, 5, 6, 7)
+WAIT_SLOT = 4
+SEND_SLOT = 2
+VMEM_LIMIT = 60 * 2**20
 AXES = ("seq_0", "seq_1", "seq_2", "res")
 SEQ = AXES[:3]
 MESH = pl.DeviceIdType.MESH
@@ -40,11 +44,11 @@
 
 
 def exchange_kernel(
-    align_hbm, w_proj_hbm, w_out_ref, w_head_hbm, gains_a_hbm, gains_h_hbm, masked_hbm, labels_hbm,
-    out_ref, stats_ref,
+    align_hbm, w_proj_hbm, w_out_hbm, w_head_hbm, gains_a_hbm, gains_h_hbm, masked_hbm, labels_hbm,
+    out_hbm, stats_ref,
     align_v, sendbuf, recv, outbuf, codes, codes_r, w_proj_v, w_k, w_qvg, w_out, w_head_v, w_head,
     gain_attn, gain_head, masked_v, labels_v, qz, va, sg, gated_t, k_nat, sb, nm, hi, acc, st_y, st_s,
-    load_sem, small_sem, send_sem, recv_sem, ysend_sem, yrecv_sem, code_sem, csend_sem, ar_sem, ars_sem,
+    load_sem, small_sem, send_sem, recv_sem, ysend_sem, yrecv_sem, own_sem, code_sem, csend_sem, ar_sem, ars_sem,
 ):
     x, z, core, y = (lax.axis_index(a) for a in AXES)
     me = (x * 4 + z) * 2 + core
@@ -82,7 +86,7 @@
         for n, (src, dst) in enumerate(
             (
                 (masked_hbm, masked_v), (labels_hbm, labels_v), (w_proj_hbm, w_proj_v),
-                (w_out_ref, w_out), (w_head_hbm, w_head_v),
+                (w_out_hbm, w_out), (w_head_hbm, w_head_v),
                 (gains_a_hbm, gain_attn), (gains_h_hbm, gain_head),
             )
         )
@@ -205,10 +209,12 @@
         for k in range(1, NRES):
             dst = lax.rem(y + k, NRES)
             pltpu.make_async_remote_copy(
-                outbuf.at[c, pl.ds(pl.multiple_of(dst * 128, 128), 128)], out_ref.at[y, c],
+                outbuf.at[c, pl.ds(pl.multiple_of(dst * 128, 128), 128)], out_hbm.at[y, c],
                 ysend_sem, yrecv_sem, device_id=res_device(k), device_id_type=MESH,
             ).start()
-        out_ref[y, c] = outbuf[c, pl.ds(pl.multiple_of(y * 128, 128), 128)]
+        pltpu.make_async_copy(
+            outbuf.at[c, pl.ds(pl.multiple_of(y * 128, 128), 128)], out_hbm.at[y, c], own_sem
+        ).start()
 
     def score(p, h):
         sb[h % 2] = dot(k_nat[p], qz[p, h])
@@ -221,14 +227,22 @@
 
     def body(c, p, following, live):
         slots = [[] for _ in range(HEADS)]
+        last = c - 1 if live is None else jnp.maximum(c - 1, 0)
+        for slot, piece in zip(AFTER_SLOTS, after(last, 1 - p, live)):
+            slots[slot].append(piece)
         if following is not None:
-            arrived(following)
-            for slot, piece in enumerate(before(following, 1 - p)):
+            for slot, piece in zip(BEFORE_SLOTS, before(following, 1 - p)):
                 slots[slot].append(piece)
-        last = c - 1 if live is None else jnp.maximum(c - 1, 0)
-        for slot, piece in zip((0, 1, 3, 4, 6), after(last, 1 - p, live)):
-            slots[slot].append(piece)
         for h in range(HEADS):
+            if h == SEND_SLOT:
+                if live is None:
+                    send_out(last)
+                else:
+                    @pl.when(live)
+                    def _():
+                        send_out(last)
+            if h == WAIT_SLOT and following is not None:
+                arrived(following)
             if h + 1 < HEADS:
                 score(p, h + 1)
             for piece in slots[h]:
@@ -236,12 +250,6 @@
             if h + 1 == HEADS and following is not None:
                 score(1 - p, 0)
             attend(p, h)
-        if live is None:
-            send_out(last)
-        else:
-            @pl.when(live)
-            def _():
-                send_out(last)
 
     arrived(0)
     for piece in before(0, 0):
@@ -264,49 +272,59 @@
 
     total_count = jnp.sum(acc[pl.ds(8, 8)], axis=0, keepdims=True)
     first = lax.broadcasted_iota(jnp.int32, (8, 128), 0) == 0
-    st_y[y] = jnp.where(first, acc[pl.ds(0, 1)], total_count)
+    st_s[me] = jnp.where(first, acc[pl.ds(0, 1)], total_count)
+    for i in range(1, NSEQ):
+        pltpu.make_async_remote_copy(
+            st_s.at[me], st_s.at[me], ars_sem.at[0], ar_sem.at[0],
+            device_id=seq_device(i), device_id_type=MESH,
+        ).start()
+    others = st_s.at[pl.ds(0, NSEQ - 1)]
+    pltpu.make_async_copy(others, others, ar_sem.at[0]).wait()
+    st_y[y] = jnp.sum(st_s[...], axis=0)
     for k in range(1, NRES):
         pltpu.make_async_remote_copy(
-            st_y.at[y], st_y.at[y], ars_sem.at[0], ar_sem.at[0],
+            st_y.at[y], st_y.at[y], ars_sem.at[1], ar_sem.at[1],
             device_id=res_device(k), device_id_type=MESH,
         ).start()
-    pltpu.make_async_copy(st_y.at[pl.ds(0, 3)], st_y.at[pl.ds(0, 3)], ar_sem.at[0]).wait()
-    st_s[me] = (st_y[0] + st_y[1]) + (st_y[2] + st_y[3])
-
-    for i in range(1, NSEQ):
-        pltpu.make_async_remote_copy(
-            st_s.at[me], st_s.at[me], ars_sem.at[1], ar_sem.at[1],
-            device_id=seq_device(i), device_id_type=MESH,
-        ).start()
-
-    pltpu.make_async_copy(st_s.at[pl.ds(0, NSEQ - 1)], st_s.at[pl.ds(0, NSEQ - 1)], ar_sem.at[1]).wait()
-    sums = jnp.sum(jnp.sum(st_s[...], axis=0), axis=1, keepdims=True)
+    three = st_y.at[pl.ds(0, 3)]
+    pltpu.make_async_copy(three, three, ar_sem.at[1]).wait()
+    sums = jnp.sum((st_y[0] + st_y[1]) + (st_y[2] + st_y[3]), axis=1, keepdims=True)
     stats_ref[...] = jnp.broadcast_to(sums, (8, 128))
 
-    pltpu.make_async_copy(st_y.at[pl.ds(0, 3)], st_y.at[pl.ds(0, 3)], ars_sem.at[0]).wait()
-    pltpu.make_async_copy(st_s.at[pl.ds(0, NSEQ - 1)], st_s.at[pl.ds(0, NSEQ - 1)], ars_sem.at[1]).wait()
+    pltpu.make_async_copy(others, others, ars_sem.at[0]).wait()
+    pltpu.make_async_copy(three, three, ars_sem.at[1]).wait()
     pltpu.make_async_copy(codes_r.at[pl.ds(0, 3)], codes_r.at[pl.ds(0, 3)], csend_sem).wait()
     sent = sendbuf.at[pl.ds(0, NSEQ - 1)]
     pltpu.make_async_copy(sent, sent, send_sem).wait()
-    three = out_ref.at[pl.ds(0, 3)]
+    pltpu.make_async_copy(out_hbm.at[0], out_hbm.at[0], own_sem).wait()
+    three = out_hbm.at[pl.ds(0, 3)]
     pltpu.make_async_copy(three, three, ysend_sem).wait()
     pltpu.make_async_copy(three, three, yrecv_sem).wait()
 
 
-def finish_kernel(part_ref, stats_ref, out_hbm, loss_ref, share_ref, moved, sem):
-    copies = []
-    for g in range(128 // ROWS):
-        span = pl.ds(ROWS * g, ROWS)
-        for b in range(NRES):
-            moved[span, b] = jnp.swapaxes(part_ref[b, :, span], 0, 1)
-        copies.append(pltpu.make_async_copy(moved.at[span], out_hbm.at[span], sem.at[g]))
-        copies[-1].start()
+def finish_kernel(part_hbm, stats_ref, out_hbm, loss_ref, share_ref, part, moved, in_sem, out_sem):
+    spans = [pl.ds(ROWS * g, ROWS) for g in range(128 // ROWS)]
+    reads = [
+        pltpu.make_async_copy(part_hbm.at[:, :, span], part.at[:, :, span], in_sem.at[g])
+        for g, span in enumerate(spans)
+    ]
+    writes = [
+        pltpu.make_async_copy(moved.at[span], out_hbm.at[span], out_sem.at[g])
+        for g, span in enumerate(spans)
+    ]
+    for read in reads:
+        read.start()
     loss_sum = stats_ref[0, 0]
     mask_count = stats_ref[1, 0]
     loss_ref[0, 0] = loss_sum / (1.0 + mask_count)
     share_ref[0, 0] = mask_count * (1.0 / 1048576)
-    for copy in copies:
-        copy.wait()
+    for read, write, span in zip(reads, writes, spans):
+        read.wait()
+        for b in range(NRES):
+            moved[span, b] = jnp.swapaxes(part[b, :, span], 0, 1)
+        write.start()
+    for write in writes:
+        write.wait()
 
 
 def on_device(alignment, gain_attn, w_proj, w_out, gain_head, w_head, masked, labels):
@@ -320,7 +338,7 @@
             jax.ShapeDtypeStruct((8, 128), F32),
         ),
         in_specs=[hbm] * 8,
-        out_specs=(vmem, vmem),
+        out_specs=(hbm, vmem),
         scratch_shapes=[
             pltpu.VMEM((ROWS, S, C), BF),
             pltpu.VMEM((NSEQ, COLS, ROWS, C), BF),
@@ -349,7 +367,7 @@
             pltpu.VMEM((16, 128), F32),
             pltpu.VMEM((NRES, 8, 128), F32),
             pltpu.VMEM((NSEQ, 8, 128), F32),
-            dma((4,)), dma((7,)), dma, dma((COLS,)), dma, dma, dma, dma, dma((2,)), dma((2,)),
+            dma((4,)), dma((7,)), dma, dma((COLS,)), dma, dma, dma, dma, dma, dma((2,)), dma((2,)),
         ],
         compiler_params=pltpu.CompilerParams(
             collective_id=0, has_side_effects=True, vmem_limit_bytes=VMEM_LIMIT
@@ -367,10 +385,15 @@
             jax.ShapeDtypeStruct((1, 1), F32),
             jax.ShapeDtypeStruct((1, 1), F32),
         ),
-        in_specs=[vmem, smem],
+        in_specs=[hbm, smem],
         out_specs=(hbm, smem, smem),
-        scratch_shapes=[pltpu.VMEM((128, NRES, COLS, C), BF), dma((128 // ROWS,))],
-        compiler_params=pltpu.CompilerParams(vmem_limit_bytes=16 * 2**20),
+        scratch_shapes=[
+            pltpu.VMEM((NRES, COLS, 128, C), BF),
+            pltpu.VMEM((128, NRES, COLS, C), BF),
+            dma((128 // ROWS,)),
+            dma((128 // ROWS,)),
+        ],
+        compiler_params=pltpu.CompilerParams(vmem_limit_bytes=60 * 2**20),
         name="finish",
     )(parts, stats)
     return updated, loss.reshape(()), share.reshape(())

time: 87.5 us -> 77.3 us (0.88)
  local copies, waits for them, and re-layouts: 5.52 us -> 0 us
  Pallas kernels: 80.8 us -> 76.3 us
    pallas_call x1, Pallas kernels: 77.5 us -> 71.6 us  [on_device(): pl.pallas_call(exchange_kernel, out_shape=(jax.ShapeDtypeStruct((NRES, CO...]
    unnamed x14 -> x0, local copies, waits for them, and re-layouts: 5.52 us -> none
    pallas_call x1, Pallas kernels: 3.34 us -> 4.77 us  [on_device(): pl.pallas_call(finish_kernel, out_shape=(jax.ShapeDtypeStruct((128, NRES,...]
where the time goes in v3:
time: 77.3 us; the launch traced here: 77.2 us
  Pallas kernels  76.3 us (99%)
  between operations  0.8 us (1%)
    pallas_call x1, Pallas kernels, on_device(): pl.pallas_call(exchange_kernel, out_shape=(jax.ShapeDtypeStruct((NRES, CO...  71.6 us
    pallas_call x1, Pallas kernels, on_device(): pl.pallas_call(finish_kernel, out_shape=(jax.ShapeDtypeStruct((128, NRES,...  4.77 us

profile of v3, /device:TPU:1, one launch (start us, length us, event | category | flops | bytes accessed | tf_op | source)
XLA Modules:
  0.0 77.2 jit_solution(3481381013833517327)
XLA Ops:
  0.6 71.6 %exchange.1 = (bf16[4,16,128,256]{3,2,1,0:T(8,128)(2,1)}, f32[8,128]{1,0:T(8,128)}) custom-call(bf16[16,1,512,256]{3,2,1,0:T(8,128)(2,1)} %align_hbm.1, bf16[256,4,256]{2,1,0:T(4,128)(2,1)} %w_proj_hbm.1, bf16[256,256]{1,0:T(8,128)(2,1)} %w_out_hbm.1, bf16[23,256]{1,0:T(8,128)(2,1)} %bitcast.9, f32[1,256]{1,0:T(1,128)} %bitcast.10, f32[1,256]{1,0:T(1,128)} %bitcast.11, ...), custom_call_target="tpu_custom_call" | custom-call | tf_op jit(solution)/shard_map/exchange/pallas_call | solution.py:334
  72.2 4.8 %finish.1 = (bf16[128,4,16,256]{3,2,1,0:T(8,128)(2,1)}, f32[1,1]{1,0:T(1,128)}, f32[1,1]{1,0:T(1,128)}) custom-call(bf16[4,16,128,256]{3,2,1,0:T(8,128)(2,1)} %get-tuple-element.8.part_hbm, f32[8,128]{1,0:T(8,128)} %get-tuple-element.9.stats_ref), custom_call_target="tpu_custom_call" | custom-call | tf_op jit(solution)/shard_map/finish/pallas_call | solution.py:381

commit v4 on v3

--- a/solution.py
+++ b/solution.py
@@ -19,11 +19,11 @@
 COLS = 16
 VAUG = 48
 LPAD = 32
-AFTER_SLOTS = (0, 0, 1, 2, 3)
-BEFORE_SLOTS = (4, 4, 4, 4, 5, 5, 6, 7)
-WAIT_SLOT = 4
-SEND_SLOT = 2
-VMEM_LIMIT = 60 * 2**20
+AFTER_SLOTS = (0, 0, 2, 3, 4)
+BEFORE_SLOTS = (5, 5, 5, 5, 6, 6, 6, 7)
+WAIT_SLOT = 5
+SEND_SLOT = 1
+VMEM_LIMIT = 48 * 2**20
 AXES = ("seq_0", "seq_1", "seq_2", "res")
 SEQ = AXES[:3]
 MESH = pl.DeviceIdType.MESH
@@ -48,7 +48,7 @@
     out_hbm, stats_ref,
     align_v, sendbuf, recv, outbuf, codes, codes_r, w_proj_v, w_k, w_qvg, w_out, w_head_v, w_head,
     gain_attn, gain_head, masked_v, labels_v, qz, va, sg, gated_t, k_nat, sb, nm, hi, acc, st_y, st_s,
-    load_sem, small_sem, send_sem, recv_sem, ysend_sem, yrecv_sem, own_sem, code_sem, csend_sem, ar_sem, ars_sem,
+    load_sem, small_sem, send_sem, recv_sem, ysend_sem, yrecv_sem, code_sem, csend_sem, ar_sem, ars_sem,
 ):
     x, z, core, y = (lax.axis_index(a) for a in AXES)
     me = (x * 4 + z) * 2 + core
@@ -212,9 +212,7 @@
                 outbuf.at[c, pl.ds(pl.multiple_of(dst * 128, 128), 128)], out_hbm.at[y, c],
                 ysend_sem, yrecv_sem, device_id=res_device(k), device_id_type=MESH,
             ).start()
-        pltpu.make_async_copy(
-            outbuf.at[c, pl.ds(pl.multiple_of(y * 128, 128), 128)], out_hbm.at[y, c], own_sem
-        ).start()
+        out_hbm[y, c] = outbuf[c, pl.ds(pl.multiple_of(y * 128, 128), 128)]
 
     def score(p, h):
         sb[h % 2] = dot(k_nat[p], qz[p, h])
@@ -296,35 +294,25 @@
     pltpu.make_async_copy(codes_r.at[pl.ds(0, 3)], codes_r.at[pl.ds(0, 3)], csend_sem).wait()
     sent = sendbuf.at[pl.ds(0, NSEQ - 1)]
     pltpu.make_async_copy(sent, sent, send_sem).wait()
-    pltpu.make_async_copy(out_hbm.at[0], out_hbm.at[0], own_sem).wait()
     three = out_hbm.at[pl.ds(0, 3)]
     pltpu.make_async_copy(three, three, ysend_sem).wait()
     pltpu.make_async_copy(three, three, yrecv_sem).wait()
 
 
-def finish_kernel(part_hbm, stats_ref, out_hbm, loss_ref, share_ref, part, moved, in_sem, out_sem):
-    spans = [pl.ds(ROWS * g, ROWS) for g in range(128 // ROWS)]
-    reads = [
-        pltpu.make_async_copy(part_hbm.at[:, :, span], part.at[:, :, span], in_sem.at[g])
-        for g, span in enumerate(spans)
-    ]
-    writes = [
-        pltpu.make_async_copy(moved.at[span], out_hbm.at[span], out_sem.at[g])
-        for g, span in enumerate(spans)
-    ]
-    for read in reads:
-        read.start()
+def finish_kernel(part_ref, stats_ref, out_hbm, loss_ref, share_ref, moved, sem):
+    copies = []
+    for g in range(128 // ROWS):
+        span = pl.ds(ROWS * g, ROWS)
+        for b in range(NRES):
+            moved[span, b] = jnp.swapaxes(part_ref[b, :, span], 0, 1)
+        copies.append(pltpu.make_async_copy(moved.at[span], out_hbm.at[span], sem.at[g]))
+        copies[-1].start()
     loss_sum = stats_ref[0, 0]
     mask_count = stats_ref[1, 0]
     loss_ref[0, 0] = loss_sum / (1.0 + mask_count)
     share_ref[0, 0] = mask_count * (1.0 / 1048576)
-    for read, write, span in zip(reads, writes, spans):
-        read.wait()
-        for b in range(NRES):
-            moved[span, b] = jnp.swapaxes(part[b, :, span], 0, 1)
-        write.start()
-    for write in writes:
-        write.wait()
+    for copy in copies:
+        copy.wait()
 
 
 def on_device(alignment, gain_attn, w_proj, w_out, gain_head, w_head, masked, labels):
@@ -338,7 +326,7 @@
             jax.ShapeDtypeStruct((8, 128), F32),
         ),
         in_specs=[hbm] * 8,
-        out_specs=(hbm, vmem),
+        out_specs=(vmem, vmem),
         scratch_shapes=[
             pltpu.VMEM((ROWS, S, C), BF),
             pltpu.VMEM((NSEQ, COLS, ROWS, C), BF),
@@ -367,15 +355,20 @@
             pltpu.VMEM((16, 128), F32),
             pltpu.VMEM((NRES, 8, 128), F32),
             pltpu.VMEM((NSEQ, 8, 128), F32),
-            dma((4,)), dma((7,)), dma, dma((COLS,)), dma, dma, dma, dma, dma, dma((2,)), dma((2,)),
+            dma((4,)), dma((7,)), dma, dma((COLS,)), dma, dma, dma, dma, dma((2,)), dma((2,)),
         ],
         compiler_params=pltpu.CompilerParams(
             collective_id=0, has_side_effects=True, vmem_limit_bytes=VMEM_LIMIT
         ),
         name="exchange",
     )(
-        alignment, w_proj, w_out, w_head.T, gain_attn.reshape(1, C), gain_head.reshape(1, C),
-        jnp.transpose(masked, (1, 2, 0)), jnp.transpose(labels, (1, 2, 0)),
+        *(
+            pltpu.with_memory_space_constraint(array, pltpu.HBM)
+            for array in (
+                alignment, w_proj, w_out, w_head.T, gain_attn.reshape(1, C), gain_head.reshape(1, C),
+                jnp.transpose(masked, (1, 2, 0)), jnp.transpose(labels, (1, 2, 0)),
+            )
+        )
     )
     smem = pl.BlockSpec(memory_space=pltpu.SMEM)
     updated, loss, share = pl.pallas_call(
@@ -385,15 +378,13 @@
             jax.ShapeDtypeStruct((1, 1), F32),
             jax.ShapeDtypeStruct((1, 1), F32),
         ),
-        in_specs=[hbm, smem],
+        in_specs=[vmem, smem],
         out_specs=(hbm, smem, smem),
         scratch_shapes=[
-            pltpu.VMEM((NRES, COLS, 128, C), BF),
             pltpu.VMEM((128, NRES, COLS, C), BF),
             dma((128 // ROWS,)),
-            dma((128 // ROWS,)),
         ],
-        compiler_params=pltpu.CompilerParams(vmem_limit_bytes=60 * 2**20),
+        compiler_params=pltpu.CompilerParams(vmem_limit_bytes=16 * 2**20),
         name="finish",
     )(parts, stats)
     return updated, loss.reshape(()), share.reshape(())

time: 77.3 us -> 75 us (0.970)
  Pallas kernels: 76.3 us -> 74.1 us
    pallas_call x1, Pallas kernels: 4.77 us -> 3.33 us  [on_device(): pl.pallas_call(finish_kernel, out_shape=(jax.ShapeDtypeStruct((128, NRES,...]
    pallas_call x1, Pallas kernels: 71.6 us -> 70.7 us  [on_device(): pl.pallas_call(exchange_kernel, out_shape=(jax.ShapeDtypeStruct((NRES, CO...]
where the time goes in v4:
time: 75 us; the launch traced here: 74.9 us
  Pallas kernels  74.1 us (99%)
  between operations  0.8 us (1%)
    pallas_call x1, Pallas kernels, on_device(): pl.pallas_call(exchange_kernel, out_shape=(jax.ShapeDtypeStruct((NRES, CO...  70.7 us
    pallas_call x1, Pallas kernels, on_device(): pl.pallas_call(finish_kernel, out_shape=(jax.ShapeDtypeStruct((128, NRES,...  3.33 us

profile of v4, /device:TPU:1, one launch (start us, length us, event | category | flops | bytes accessed | tf_op | source)
XLA Modules:
  0.0 74.9 jit_solution(13189912131385240089)
XLA Ops:
  0.6 70.7 %exchange.1 = (bf16[4,16,128,256]{3,2,1,0:T(8,128)(2,1)S(1)}, f32[8,128]{1,0:T(8,128)S(1)}) custom-call(bf16[16,1,512,256]{3,2,1,0:T(8,128)(2,1)} %align_hbm.1, bf16[256,4,256]{2,1,0:T(4,128)(2,1)} %w_proj_hbm.1, bf16[256,256]{1,0:T(8,128)(2,1)} %w_out_hbm.1, bf16[23,256]{1,0:T(8,128)(2,1)} %bitcast.9, f32[1,256]{1,0:T(1,128)} %bitcast.10, ...), custom_call_target="tpu_custom_call" | custom-call | tf_op jit(solution)/shard_map/exchange/pallas_call | solution.py:322
  71.4 3.3 %finish.1 = (bf16[128,4,16,256]{3,2,1,0:T(8,128)(2,1)}, f32[1,1]{1,0:T(1,128)}, f32[1,1]{1,0:T(1,128)}) custom-call(bf16[4,16,128,256]{3,2,1,0:T(8,128)(2,1)S(1)} %get-tuple-element.8.part_ref, f32[8,128]{1,0:T(8,128)S(1)} %get-tuple-element.9.stats_ref), custom_call_target="tpu_custom_call" | custom-call | tf_op jit(solution)/shard_map/finish/pallas_call | solution.py:374

commit v5 on v4

--- a/solution.py
+++ b/solution.py
@@ -32,6 +32,13 @@
 QSCALE = HEAD_DIM ** (-0.5) * math.log2(math.e)
 
 
+def hops(i):
+    return min(i // 8, 4 - i // 8) + min(i // 2 % 4, 4 - i // 2 % 4)
+
+
+FAR_FIRST = sorted(range(1, NSEQ), key=hops, reverse=True)
+
+
 def normed_rows(values, gain):
     mean = jnp.mean(values, axis=-1, keepdims=True)
     centred = values - mean
@@ -69,10 +76,10 @@
 
     barrier = pltpu.get_barrier_semaphore()
 
-    for i in range(1, NSEQ):
+    for i in FAR_FIRST:
         pl.semaphore_signal(barrier, inc=1, device_id=seq_device(i), device_id_type=MESH)
 
-    for k in range(1, NRES):
+    for k in (2, 1, 3):
         pl.semaphore_signal(barrier, inc=1, device_id=res_device(k), device_id_type=MESH)
 
     loads = [
@@ -113,7 +120,7 @@
 
     pl.semaphore_wait(barrier, NSEQ - 1 + NRES - 1)
 
-    for k in range(1, NRES):
+    for k in (2, 1, 3):
         pltpu.make_async_remote_copy(
             codes.at[lax.rem(y + k, NRES)], codes_r.at[y], csend_sem, code_sem,
             device_id=res_device(k), device_id_type=MESH,
@@ -121,7 +128,7 @@
 
     @pl.loop(0, COLS)
     def _(c):
-        for i in range(1, NSEQ):
+        for i in FAR_FIRST:
             pltpu.make_async_remote_copy(
                 sendbuf.at[seq_index(i), c], recv.at[c, me],
                 send_sem, recv_sem.at[c], device_id=seq_device(i), device_id_type=MESH,
@@ -206,7 +213,7 @@
         return [project(0), project(256), norm(0), norm(256), loss]
 
     def send_out(c):
-        for k in range(1, NRES):
+        for k in (2, 1, 3):
             dst = lax.rem(y + k, NRES)
             pltpu.make_async_remote_copy(
                 outbuf.at[c, pl.ds(pl.multiple_of(dst * 128, 128), 128)], out_hbm.at[y, c],
@@ -271,7 +278,7 @@
     total_count = jnp.sum(acc[pl.ds(8, 8)], axis=0, keepdims=True)
     first = lax.broadcasted_iota(jnp.int32, (8, 128), 0) == 0
     st_s[me] = jnp.where(first, acc[pl.ds(0, 1)], total_count)
-    for i in range(1, NSEQ):
+    for i in FAR_FIRST:
         pltpu.make_async_remote_copy(
             st_s.at[me], st_s.at[me], ars_sem.at[0], ar_sem.at[0],
             device_id=seq_device(i), device_id_type=MESH,
@@ -279,7 +286,7 @@
     others = st_s.at[pl.ds(0, NSEQ - 1)]
     pltpu.make_async_copy(others, others, ar_sem.at[0]).wait()
     st_y[y] = jnp.sum(st_s[...], axis=0)
-    for k in range(1, NRES):
+    for k in (2, 1, 3):
         pltpu.make_async_remote_copy(
             st_y.at[y], st_y.at[y], ars_sem.at[1], ar_sem.at[1],
             device_id=res_device(k), device_id_type=MESH,

time: 75 us -> 74.2 us (0.989)
  Pallas kernels: 74.1 us -> 73.1 us
    pallas_call x1, Pallas kernels: 70.7 us -> 69.7 us  [on_device(): pl.pallas_call(exchange_kernel, out_shape=(jax.ShapeDtypeStruct((NRES, CO...]
where the time goes in v5:
time: 74.2 us; the launch traced here: 73.9 us
  Pallas kernels  73.1 us (99%)
  between operations  0.8 us (1%)
    pallas_call x1, Pallas kernels, on_device(): pl.pallas_call(exchange_kernel, out_shape=(jax.ShapeDtypeStruct((NRES, CO...  69.7 us
    pallas_call x1, Pallas kernels, on_device(): pl.pallas_call(finish_kernel, out_shape=(jax.ShapeDtypeStruct((128, NRES,...  3.33 us

profile of v5, /device:TPU:1, one launch (start us, length us, event | category | flops | bytes accessed | tf_op | source)
XLA Modules:
  0.0 73.9 jit_solution(11057120295974144911)
XLA Ops:
  0.6 69.7 %exchange.1 = (bf16[4,16,128,256]{3,2,1,0:T(8,128)(2,1)S(1)}, f32[8,128]{1,0:T(8,128)S(1)}) custom-call(bf16[16,1,512,256]{3,2,1,0:T(8,128)(2,1)} %align_hbm.1, bf16[256,4,256]{2,1,0:T(4,128)(2,1)} %w_proj_hbm.1, bf16[256,256]{1,0:T(8,128)(2,1)} %w_out_hbm.1, bf16[23,256]{1,0:T(8,128)(2,1)} %bitcast.9, f32[1,256]{1,0:T(1,128)} %bitcast.10, ...), custom_call_target="tpu_custom_call" | custom-call | tf_op jit(solution)/shard_map/exchange/pallas_call | solution.py:329
  70.4 3.3 %finish.1 = (bf16[128,4,16,256]{3,2,1,0:T(8,128)(2,1)}, f32[1,1]{1,0:T(1,128)}, f32[1,1]{1,0:T(1,128)}) custom-call(bf16[4,16,128,256]{3,2,1,0:T(8,128)(2,1)S(1)} %get-tuple-element.8.part_ref, f32[8,128]{1,0:T(8,128)S(1)} %get-tuple-element.9.stats_ref), custom_call_target="tpu_custom_call" | custom-call | tf_op jit(solution)/shard_map/finish/pallas_call | solution.py:381
